TPU v7x, 32 devices: a whole 2x2x4 slice. The times are simulated.
32 devices in a mesh: grp: 2 (over y), kvp: 4 (over x, core), tp: 4 (over z).
Axes of the slice: x: 2, y: 2, z: 4, core: 2. Of those that a mesh axis runs over, the one named last changes fastest.
Arguments:
- hidden_in: bfloat16 [16, 7168], P('grp'), parts along dimension 0, may hold values from -3 to 3
- queries_nope: bfloat16 [16, 128, 128], P('grp', ('kvp', 'tp')), parts along dimension 0, may hold values from -6 to 6
- queries_rope: bfloat16 [16, 128, 64], P('grp', ('kvp', 'tp')), parts along dimension 0, may hold values from -26 to 26
- cache: bfloat16 [16, 1536, 576], P('grp', 'kvp'), parts along dimension 0, may hold values from -20 to 20
- lengths: int32 [16], P('grp'), parts along dimension 0, may hold values from 128 to 1536, as said below
- w_uk: bfloat16 [128, 128, 512], P(('kvp', 'tp')), may hold values from -0.5 to 0.5
- w_uv: bfloat16 [128, 512, 128], P(('kvp', 'tp')), may hold values from -0.25 to 0.25
- w_out: bfloat16 [16384, 7168], P(('kvp', 'tp')), may hold values from -0.0625 to 0.0625
- norm_gain: float32 [7168], replicated, may hold values from 0.25 to 1.75
- w_gate: bfloat16 [7168, 18432], P(None, ('kvp', 'tp')), may hold values from -0.0625 to 0.0625
- w_up: bfloat16 [7168, 18432], P(None, ('kvp', 'tp')), may hold values from -0.0625 to 0.0625
- w_down: bfloat16 [18432, 7168], P(('kvp', 'tp')), may hold values from -0.0625 to 0.0625
Outputs:
- layer_out: bfloat16 [16, 7168], P('grp', ('kvp', 'tp')), parts along dimension 0
There are 2 independent parts, one for each index of `grp`. A program takes and returns all parts, laid end to end along the dimension named above; an argument that names none is the same for every part. Nothing has to cross between parts.
Inputs may be any that keep to these rules, and one draw needn't show every extreme that they name: `lengths`: every length is a multiple of 128; in every draw some request has the full 1536.
All inputs are finite; a program needn't handle non-finite values.
Results may differ from a plain program's by a relative error of at most 0.04.
Values may be sent and summed in bfloat16 or wider, within the bound.
A program may use at most 128 MiB of HBM per device.

v0:
```python
import jax
import jax.numpy as jnp
from jax import lax
from jax.sharding import PartitionSpec as P


def project(o_lat, w_uv, w_out):
    head_out = jnp.einsum("bhl,hle->bhe", o_lat, w_uv, preferred_element_type=jnp.float32).astype(
        jnp.bfloat16
    )
    return jnp.dot(
        head_out.reshape(head_out.shape[0], -1), w_out, preferred_element_type=jnp.float32
    )


def per_device(
    hidden_in,
    queries_nope,
    queries_rope,
    cache,
    lengths,
    w_uk,
    w_uv,
    w_out,
    norm_gain,
    w_gate,
    w_up,
    w_down,
):
    batch, heads_dev, head_dim = queries_nope.shape
    latent = w_uk.shape[2]
    ctx_dev = cache.shape[1]
    groups = lax.axis_size("kvp")
    score_scale = float(head_dim + queries_rope.shape[2]) ** (-0.5)
    q_lat = jnp.einsum(
        "bhd,hdl->bhl", queries_nope, w_uk, preferred_element_type=jnp.float32
    ).astype(jnp.bfloat16)
    q_lat_all, rope_all = (
        lax.all_gather(q_lat, "kvp", axis=1, tiled=True),
        lax.all_gather(queries_rope, "kvp", axis=1, tiled=True),
    )
    q_full = jnp.concatenate([q_lat_all, rope_all], axis=2)
    scores = (
        jnp.einsum("bhc,btc->bht", q_full, cache, preferred_element_type=jnp.float32) * score_scale
    )
    offset = lax.axis_index("kvp") * ctx_dev
    visible = ((offset + jnp.arange(ctx_dev, dtype=jnp.int32))[None, :] < lengths[:, None])[
        :, None, :
    ]
    masked = jnp.where(visible, scores, jnp.float32(-1e30))
    block_max = jnp.max(masked, axis=2)
    exponent = jnp.where(visible, jnp.exp(masked - block_max[..., None]), jnp.float32(0.0))
    guarded = jnp.maximum(jnp.sum(exponent, axis=2), 1.0)
    log_total = block_max + jnp.log(guarded)
    weights = (exponent / guarded[..., None]).astype(jnp.bfloat16)
    partial_value = jnp.einsum("bht,btc->bhc", weights, cache, preferred_element_type=jnp.float32)[
        ..., :latent
    ]
    blocks = partial_value.reshape(batch, groups, heads_dev, latent)
    block_logs = log_total.reshape(batch, groups, heads_dev)
    part_blocks = lax.all_to_all(
        blocks.astype(jnp.bfloat16), "kvp", split_axis=1, concat_axis=1, tiled=True
    ).astype(blocks.dtype)
    part_logs = lax.all_to_all(
        block_logs.astype(jnp.bfloat16), "kvp", split_axis=1, concat_axis=1, tiled=True
    ).astype(block_logs.dtype)
    highest = jnp.max(part_logs, axis=1)
    overall = highest + jnp.log(jnp.sum(jnp.exp(part_logs - highest[:, None, :]), axis=1))
    scaled = jnp.exp(part_logs - overall[:, None, :])[..., None] * part_blocks
    o_lat = jnp.sum(scaled, axis=1).astype(jnp.bfloat16)
    attention = project(o_lat, w_uv, w_out)
    model_width = norm_gain.shape[0]
    share_width = model_width // lax.axis_size(("kvp", "tp"))
    share_start = lax.axis_index(("kvp", "tp")) * share_width
    attn_whole = lax.psum(attention, ("kvp", "tp"))
    residual = hidden_in.astype(jnp.float32) + attn_whole
    mean_square = jnp.mean(residual * residual, axis=1)
    normed = (residual * lax.rsqrt(mean_square + 1e-06)[:, None] * norm_gain[None, :]).astype(
        jnp.bfloat16
    )
    residual_share = lax.dynamic_slice_in_dim(residual, share_start, share_width, 1)
    gate_proj = jnp.dot(normed, w_gate, preferred_element_type=jnp.float32)
    up_proj = jnp.dot(normed, w_up, preferred_element_type=jnp.float32)
    act = (jax.nn.silu(gate_proj) * up_proj).astype(jnp.bfloat16)
    ffn_terms = jnp.dot(act, w_down, preferred_element_type=jnp.float32)
    ffn_share = lax.psum_scatter(ffn_terms, ("kvp", "tp"), scatter_dimension=1, tiled=True)
    return (residual_share + ffn_share).astype(jnp.bfloat16)


def solution(mesh):
    placed = (
        P("grp", None),
        P("grp", ("kvp", "tp"), None),
        P("grp", ("kvp", "tp"), None),
        P("grp", "kvp", None),
        P("grp"),
        P(("kvp", "tp"), None, None),
        P(("kvp", "tp"), None, None),
        P(("kvp", "tp"), None),
        P(),
        P(None, ("kvp", "tp")),
        P(None, ("kvp", "tp")),
        P(("kvp", "tp"), None),
    )
    return jax.shard_map(
        per_device, mesh=mesh, in_specs=placed, out_specs=P("grp", ("kvp", "tp")), check_vma=False
    )
```

profile of v0, /device:TPU:0, one launch (start us, length us, event | category | flops | bytes accessed | tf_op | source)
XLA Modules:
  0.0 248.7 jit_solution(1045707272200250479)
XLA Ops:
  6.5 0.0 copy-start
  6.5 0.9 copy.24
  7.4 6.3 %all_gather.7 = bf16[8,32,64]{2,0,1:T(8,128)(2,1)S(1)} all-gather(bf16[8,8,64]{2,0,1:T(8,128)(2,1)S(1)} %copy.24), channel_id=1, replica_groups=mesh['grp'=2,'kvp'=4,'tp'=4] {'kvp'}, dimensions={1}, use_global_device_ids=true | all-gather | bytes 40960 | tf_op jit(solution)/shard_map/all_gather | solution.py:40
  13.7 1.5 fusion.2
  15.2 6.3 %all_gather.6 = bf16[8,32,512]{2,0,1:T(8,128)(2,1)S(1)} all-gather(bf16[8,8,512]{2,0,1:T(8,128)(2,1)S(1)} %fusion.2), channel_id=1, replica_groups=mesh['grp'=2,'kvp'=4,'tp'=4] {'kvp'}, dimensions={1}, use_global_device_ids=true | all-gather | bytes 327680 | tf_op jit(solution)/shard_map/all_gather | solution.py:39
  21.5 0.1 copy.25
  21.6 0.7 broadcast_compare_fusion
  22.3 0.0 copy-done
  22.3 0.7 fusion.31
  23.0 0.0 copy-start.3
  23.0 0.7 copy-done.3
  23.8 0.2 fusion.8
  24.0 0.6 add_convert_fusion.1
  24.6 0.8 convert_element_type.50
  25.3 0.6 copy.27
  25.9 3.2 %all-to-all-start = ((bf16[8,4,8]{2,0,1:T(8,128)(2,1)}), bf16[8,4,8]{2,0,1:T(8,128)(2,1)S(1)}, u32[]{:S(2)}, u32[]{:S(2)}) async-start(bf16[8,4,8]{2,0,1:T(8,128)(2,1)} %copy.27), calls=%async_computation | async-start | bytes 16384 | tf_op jit(solution)/shard_map/all_to_all | solution.py:64
  29.2 2.2 fusion.10
  31.4 0.0 copy-start.5
  31.5 0.0 copy-start.4
  31.5 0.7 copy.28
  32.2 0.8 all-to-all-done
  33.0 3.4 %all-to-all-start.1 = ((bf16[8,4,8,512]{3,2,0,1:T(8,128)(2,1)}), bf16[8,4,8,512]{3,2,0,1:T(8,128)(2,1)S(1)}, u32[]{:S(2)}, u32[]{:S(2)}) async-start(bf16[8,4,8,512]{3,2,0,1:T(8,128)(2,1)} %copy.28), calls=%async_computation.1 | async-start | bytes 524288 | tf_op jit(solution)/shard_map/all_to_all | solution.py:61
  36.4 0.0 all-reduce.2.cloned.1.call-start
  36.5 5.8 %all-to-all-done.1 = bf16[8,4,8,512]{3,2,0,1:T(8,128)(2,1)S(1)} async-done(((bf16[8,4,8,512]{3,2,0,1:T(8,128)(2,1)}), bf16[8,4,8,512]{3,2,0,1:T(8,128)(2,1)S(1)}, u32[]{:S(2)}, u32[]{:S(2)}) %all-to-all-start.1) | async-done | bytes 262176 | tf_op jit(solution)/shard_map/all_to_all | solution.py:61
  42.4 0.1 multiply_reduce_fusion
  42.5 8.4 %fusion.4 = f32[8,7168]{1,0:T(8,128)} fusion(bf16[1024,7168]{1,0:T(8,128)(2,1)} %param.19, bf16[8,512,128]{2,1,0:T(8,128)(2,1)} %param.18, bf16[8,8,512]{2,1,0:T(8,128)(2,1)S(1)} %multiply_reduce_fusion), kind=kOutput, calls=%fused_computation.9 | convolution fusion | flops 125837312 | bytes 16023552 | tf_op jit(solution)/shard_map/dot_general | solution.py:11
  50.8 0.0 all-reduce.2.cloned.1.call-update
  50.9 0.0 reduce-scatter.4.cloned.1.call-start
  50.9 89.8 %all-reduce.2.cloned.1.call-done = f32[8,7168]{1,0:T(8,128)} async-done(((f32[8,7168]{1,0:T(8,128)}), f32[8,7168]{1,0:T(8,128)}) %all-reduce.2.cloned.1.call-update) | async-done | bytes 229392 | tf_op jit(solution)/shard_map/psum | solution.py:75
  140.7 0.0 copy-done.5
  140.7 1.1 multiply_reduce_fusion.1
  141.8 0.0 copy-start.2
  141.8 0.7 copy-done.2
  142.5 0.0 copy-done.4
  142.5 8.6 %fusion.30 = f32[8,1152]{1,0:T(8,128)} fusion(bf16[7168,1152]{1,0:T(8,128)(2,1)} %param.21, f32[8,7168]{1,0:T(8,128)S(1)} %get-tuple-element.6, f32[7168]{0:T(1024)S(1)} %copy-done.4, f32[8]{0:T(128)S(1)} %add_rsqrt_fusion), kind=kOutput, calls=%fused_computation.50 | convolution fusion | flops 132292608 | bytes 16810016 | tf_op jit(solution)/shard_map/dot_general | solution.py:82
  151.1 0.0 copy-start.1
  151.1 18.6 %convolution_bitcast_fusion = f32[7168,8]{1,0:T(8,128)} fusion(bf16[1152,7168]{1,0:T(8,128)(2,1)} %param.23, bf16[7168,1152]{1,0:T(8,128)(2,1)} %param.22, f32[8,1152]{1,0:T(8,128)} %fusion.30, f32[8,7168]{1,0:T(8,128)} %copy-done.2, f32[7168]{0:T(1024)} %param.20, f32[8]{0:T(128)S(1)} %add_rsqrt_fusion), kind=kOutput, calls=%fused_computation | convolution fusion | flops 264468480 | bytes 33554464
  169.7 0.0 reduce-scatter.4.cloned.1.call-update
  169.7 69.7 %reduce-scatter.4.cloned.1.call-done = f32[448,8]{1,0:T(8,128)} async-done(((f32[7168,8]{1,0:T(8,128)}), f32[448,8]{1,0:T(8,128)}) %reduce-scatter.4.cloned.1.call-update) | async-done | bytes 14352
  239.4 1.0 copy.32
  240.4 1.4 add_convert_fusion
  241.9 0.0 copy-done.1
  (9 shorter events, 0.1 us)
Async XLA Ops:
  6.5 15.7 %copy-start = (bf16[8,384,576]{1,2,0:T(8,128)(2,1)S(1)}, bf16[8,384,576]{1,2,0:T(8,128)(2,1)}, u32[]{:S(2)}) copy-start(bf16[8,384,576]{1,2,0:T(8,128)(2,1)} %param.15) | copy-start | bytes 10616836
  23.0 0.7 copy-start.3
  25.9 7.0 %all-to-all-start = ((bf16[8,4,8]{2,0,1:T(8,128)(2,1)}), bf16[8,4,8]{2,0,1:T(8,128)(2,1)S(1)}, u32[]{:S(2)}, u32[]{:S(2)}) async-start(bf16[8,4,8]{2,0,1:T(8,128)(2,1)} %copy.27), calls=%async_computation | async-start | bytes 16384 | tf_op jit(solution)/shard_map/all_to_all | solution.py:64
  31.4 109.2 %copy-start.5 = (bf16[8,7168]{1,0:T(8,128)(2,1)S(1)}, bf16[8,7168]{1,0:T(8,128)(2,1)}, u32[]{:S(2)}) copy-start(bf16[8,7168]{1,0:T(8,128)(2,1)} %param.12) | copy-start | bytes 344068
  31.5 111.0 %copy-start.4 = (f32[7168]{0:T(1024)S(1)}, f32[7168]{0:T(1024)}, u32[]{:S(2)}) copy-start(f32[7168]{0:T(1024)} %param.20) | copy-start | bytes 86020
  33.0 9.4 %all-to-all-start.1 = ((bf16[8,4,8,512]{3,2,0,1:T(8,128)(2,1)}), bf16[8,4,8,512]{3,2,0,1:T(8,128)(2,1)S(1)}, u32[]{:S(2)}, u32[]{:S(2)}) async-start(bf16[8,4,8,512]{3,2,0,1:T(8,128)(2,1)} %copy.28), calls=%async_computation.1 | async-start | bytes 524288 | tf_op jit(solution)/shard_map/all_to_all | solution.py:61
  36.4 104.3 %all-reduce.2.cloned.1.call-start = ((), (), s32[]{:S(2)}) async-start(), calls=%async_computation.3 | async-start | bytes 458752 | tf_op jit(solution)/shard_map/psum | solution.py:75
  50.9 188.6 %reduce-scatter.4.cloned.1.call-start = ((), (), s32[]{:S(2)}) async-start(), calls=%async_computation.4 | async-start | bytes 3899392
  141.8 0.7 copy-start.2
  151.1 90.8 %copy-start.1 = (bf16[8,384,576]{1,2,0:T(8,128)(2,1)S(1)}, bf16[8,384,576]{1,2,0:T(8,128)(2,1)}, u32[]{:S(2)}) copy-start(bf16[8,384,576]{1,2,0:T(8,128)(2,1)} %param.15) | copy-start | bytes 10616836
Sparse Core Ops, SparseCore 0:
  51.0 89.6 all-reduce.1
  169.9 69.5 reduce-scatter.3
where the time goes:
time: 249 us
  waiting for transfers between devices  166 us (67%)
  matrix products  40 us (16%)
  between operations  13.5 us (5%)
  blocking collectives  12.6 us (5%)
  starting transfers between devices  6.74 us (3%)
  local copies, waits for them, and re-layouts  5.54 us (2%)
  other arithmetic  4.23 us (2%)
    psum x1, waiting for transfers between devices, per_device(): attn_whole = lax.psum(attention, ('kvp', 'tp'))  89.8 us
    unnamed x3, waiting for transfers between devices  69.7 us
    unnamed x1, matrix products  18.6 us
    dot_general x1, matrix products, per_device(): gate_proj = jnp.dot(normed, w_gate, preferred_element_type=jnp.float32)  8.58 us
    dot_general x1, matrix products, project(): jnp.dot(head_out.reshape(head_out.shape[0], -1), w_out, preferred_element...  8.36 us
    all_gather x1, blocking collectives, per_device(): lax.all_gather(queries_rope, 'kvp', axis=1, tiled=True)  6.3 us
    all_gather x1, blocking collectives, per_device(): lax.all_gather(q_lat, 'kvp', axis=1, tiled=True)  6.27 us
    all_to_all x1, waiting for transfers between devices, per_device(): lax.all_to_all(blocks.astype(jnp.bfloat16), 'kvp', split_axis=1, concat_a...  5.84 us
  transfers between devices with their start and end apart: 4, of which 4 were waited for; matrix products, arithmetic and copies ran while one was open for 1% of the time, Pallas kernels for 0%

commit v1 on v0

--- a/solution.py
+++ b/solution.py
@@ -1,6 +1,10 @@
+import functools
+
 import jax
 import jax.numpy as jnp
 from jax import lax
+from jax.experimental import pallas as pl
+from jax.experimental.pallas import tpu as pltpu
 from jax.sharding import PartitionSpec as P
 
 
@@ -13,7 +17,7 @@
     )
 
 
-def per_device(
+def plain_device(
     hidden_in,
     queries_nope,
     queries_rope,
@@ -87,6 +91,337 @@
     return (residual_share + ffn_share).astype(jnp.bfloat16)
 
 
+MESH = pl.DeviceIdType.MESH
+F32 = jnp.float32
+BF16 = jnp.bfloat16
+VMEM_BYTES = 67043328
+
+
+def layer_kernel(
+    groups, tps, share, chunk, out_rows,
+    hidden_ref, nope_ref, rope_ref, len_ref, gain_ref,
+    cache_hbm, uk_hbm, uv_hbm, wo_hbm, wg_hbm, wu_hbm, wd_hbm,
+    out_ref,
+    cache_v, uk_v, uv_v, big_v, wg_v, wu_v,
+    nope_s, qlat_s, q_send, q_all, score_s, part_send, part_all, log_send, log_all,
+    olat_s, head_s, hid_s, rs_send, rs_all, ag_send, ag_all, wide_s, norm_s, fs_send, fs_all,
+    uk_sem, cache_sem, uv_sem, wo_sem, wg_sem, wu_sem, wd_sem,
+    q_ss, q_rs, part_ss, part_rs, log_ss, log_rs, rs_ss, rs_rs, ag_ss, ag_rs, fs_ss, fs_rs,
+):
+    count = groups * tps
+    kvp = lax.axis_index("kvp")
+    tp = lax.axis_index("tp")
+    me = kvp * tps + tp
+    batch, heads, head_dim = nope_ref.shape
+    latent = uk_v.shape[2]
+    rope = rope_ref.shape[2]
+    ctx = cache_v.shape[1]
+    width = hidden_ref.shape[1]
+    chunks = width // chunk
+    per_chunk = chunk // share
+
+    def peer(index):
+        return {"kvp": index // tps, "tp": index % tps}
+
+    def load_uk():
+        return pltpu.make_async_copy(uk_hbm, uk_v, uk_sem)
+
+    def load_cache():
+        return pltpu.make_async_copy(cache_hbm, cache_v, cache_sem)
+
+    def load_uv():
+        return pltpu.make_async_copy(uv_hbm, uv_v, uv_sem)
+
+    def cols(j):
+        return pl.ds(pl.multiple_of(j * chunk, 128), chunk)
+
+    def load_wo(j):
+        return pltpu.make_async_copy(
+            wo_hbm.at[:, cols(j)], big_v.at[j, pl.ds(0, out_rows)], wo_sem.at[j]
+        )
+
+    def load_wd(j):
+        return pltpu.make_async_copy(wd_hbm.at[:, cols(j)], big_v.at[j], wd_sem.at[j])
+
+    def load_wg(j):
+        return pltpu.make_async_copy(wg_hbm.at[cols(j)], wg_v.at[cols(j)], wg_sem.at[j])
+
+    def load_wu(j):
+        return pltpu.make_async_copy(wu_hbm.at[cols(j)], wu_v.at[cols(j)], wu_sem.at[j])
+
+    load_uk().start()
+    load_cache().start()
+
+    barrier = pltpu.get_barrier_semaphore()
+
+    @pl.loop(1, count)
+    def _(d):
+        pl.semaphore_signal(
+            barrier, inc=1, device_id=peer(lax.rem(me + d, count)), device_id_type=MESH
+        )
+
+    nope_s[...] = nope_ref[...].astype(F32)
+    for s in range(count):
+        hid_s[s] = hidden_ref[:, s * share : (s + 1) * share].astype(F32)
+    load_uk().wait()
+    load_uv().start()
+
+    @pl.loop(0, chunks)
+    def _(j):
+        load_wo(j).start()
+
+    for i in range(heads):
+        qlat_s[:, i, :] = jnp.dot(
+            nope_s[:, i, :].astype(BF16), uk_v[i], preferred_element_type=F32
+        )
+    q_send[:, :, :latent] = qlat_s[...].astype(BF16)
+    q_send[:, :, latent:] = rope_ref[...]
+    pl.semaphore_wait(barrier, count - 1)
+
+    def exchange(d, source, target, ss, rs, ahead):
+        other = lax.rem(kvp + d, groups) if ahead else lax.rem(kvp + groups - d, groups)
+        return pltpu.make_async_remote_copy(
+            src_ref=source.at[other] if source is not q_send else source,
+            dst_ref=target.at[kvp if ahead else other],
+            send_sem=ss.at[d],
+            recv_sem=rs.at[kvp if ahead else other],
+            device_id={"kvp": other, "tp": tp},
+            device_id_type=MESH,
+        )
+
+    for d in range(1, groups):
+        exchange(d, q_send, q_all, q_ss, q_rs, True).start()
+
+    @pl.loop(0, chunks)
+    def _(j):
+        load_wg(j).start()
+        load_wu(j).start()
+
+    q_all[kvp] = q_send[...]
+    load_cache().wait()
+    for d in range(1, groups):
+        exchange(d, q_send, q_all, q_ss, q_rs, False).wait_recv()
+
+    scale = float(head_dim + rope) ** (-0.5)
+    rows = groups * heads
+    for b in range(batch):
+        q = q_all[:, b].astype(F32).reshape(rows, latent + rope)
+        contract = (((1,), (1,)), ((), ()))
+        score_s[b] = (
+            lax.dot_general(
+                q[:, :latent].astype(BF16), cache_v[b, :, :latent], contract,
+                preferred_element_type=F32,
+            )
+            + lax.dot_general(
+                q[:, latent:].astype(BF16), cache_v[b, :, latent:], contract,
+                preferred_element_type=F32,
+            )
+        ) * scale
+    position = kvp * ctx + lax.broadcasted_iota(jnp.int32, (rows, ctx), 1)
+    for b in range(batch):
+        visible = position < len_ref[b]
+        masked = jnp.where(visible, score_s[b], F32(-1e30))
+        top = jnp.max(masked, axis=1, keepdims=True)
+        exps = jnp.where(visible, jnp.exp(masked - top), F32(0.0))
+        guarded = jnp.maximum(jnp.sum(exps, axis=1, keepdims=True), 1.0)
+        log_total = jnp.broadcast_to(top + jnp.log(guarded), (rows, 128))
+        weights = (exps / guarded).astype(BF16)
+        part = jnp.dot(weights, cache_v[b, :, :latent], preferred_element_type=F32)
+        for g in range(groups):
+            part_send[g, b] = part[g * heads : (g + 1) * heads].astype(BF16)
+            log_send[g, b] = log_total[g * heads : (g + 1) * heads]
+
+    for d in range(1, groups):
+        exchange(d, log_send, log_all, log_ss, log_rs, True).start()
+        exchange(d, part_send, part_all, part_ss, part_rs, True).start()
+    part_all[kvp] = part_send[kvp]
+    log_all[kvp] = log_send[kvp]
+    load_uv().wait()
+    for d in range(1, groups):
+        exchange(d, log_send, log_all, log_ss, log_rs, False).wait_recv()
+        exchange(d, part_send, part_all, part_ss, part_rs, False).wait_recv()
+
+    logs = [log_all[g] for g in range(groups)]
+    highest = functools.reduce(jnp.maximum, logs)
+    overall = highest + jnp.log(sum(jnp.exp(x - highest) for x in logs))
+    factors = [jnp.exp(x - overall) for x in logs]
+    for c in range(0, latent, 128):
+        olat_s[:, :, c : c + 128] = sum(
+            factors[g] * part_all[g, :, :, c : c + 128].astype(F32) for g in range(groups)
+        )
+    for i in range(heads):
+        head_s[:, i * head_dim : (i + 1) * head_dim] = jnp.dot(
+            olat_s[:, i, :].astype(BF16), uv_v[i], preferred_element_type=F32
+        ).astype(BF16)
+
+    def scatter(d, source, target, ss, rs, ahead):
+        other = lax.rem(me + d, count) if ahead else lax.rem(me + count - d, count)
+        return pltpu.make_async_remote_copy(
+            src_ref=source.at[other] if source is not ag_send else source,
+            dst_ref=target.at[me if ahead else other],
+            send_sem=ss.at[d],
+            recv_sem=rs.at[me if ahead else other],
+            device_id=peer(other),
+            device_id_type=MESH,
+        )
+
+    def send_all(source, target, ss, rs):
+        @pl.loop(1, count)
+        def _(d):
+            scatter(d, source, target, ss, rs, True).start()
+
+    def receive_all(source, target, ss, rs):
+        @pl.loop(1, count)
+        def _(d):
+            scatter(d, source, target, ss, rs, False).wait_recv()
+
+    def sent_all(source, target, ss, rs):
+        @pl.loop(1, count)
+        def _(d):
+            scatter(d, source, target, ss, rs, True).wait_send()
+
+    @pl.loop(0, chunks)
+    def _(j):
+        load_wo(j).wait()
+        term = jnp.dot(head_s[...], big_v[j, :out_rows], preferred_element_type=F32)
+        for p in range(per_chunk):
+            rs_send[j * per_chunk + p] = term[:, p * share : (p + 1) * share].astype(BF16)
+        load_wd(j).start()
+
+    send_all(rs_send, rs_all, rs_ss, rs_rs)
+    rs_all[me] = rs_send[me]
+    receive_all(rs_send, rs_all, rs_ss, rs_rs)
+    residual = hid_s[me]
+    for s in range(count):
+        residual = residual + rs_all[s].astype(F32)
+    hid_s[me] = residual
+    ag_send[...] = residual.astype(BF16)
+    send_all(ag_send, ag_all, ag_ss, ag_rs)
+    ag_all[me] = ag_send[...]
+    receive_all(ag_send, ag_all, ag_ss, ag_rs)
+
+    square = jnp.zeros((batch, share), F32)
+    for s in range(count):
+        value = ag_all[s].astype(F32)
+        square = square + value * value
+        wide_s[:, s * share : (s + 1) * share] = value
+    mean_square = jnp.sum(square, axis=1, keepdims=True) / width
+    inverse = lax.rsqrt(mean_square + 1e-06)
+    norm_s[...] = (wide_s[...] * inverse * gain_ref[...]).astype(BF16)
+
+    def hidden_units(j, totals):
+        load_wg(j).wait()
+        load_wu(j).wait()
+        x = norm_s[:, cols(j)]
+        return (
+            totals[0] + jnp.dot(x, wg_v[cols(j)], preferred_element_type=F32),
+            totals[1] + jnp.dot(x, wu_v[cols(j)], preferred_element_type=F32),
+        )
+
+    zero = jnp.zeros((batch, wg_v.shape[1]), F32)
+    gate, up = lax.fori_loop(0, chunks, hidden_units, (zero, zero))
+    act = (gate / (1.0 + jnp.exp(-gate)) * up).astype(BF16)
+
+    @pl.loop(0, chunks)
+    def _(j):
+        load_wd(j).wait()
+        term = jnp.dot(act, big_v[j], preferred_element_type=F32)
+        for p in range(per_chunk):
+            fs_send[j * per_chunk + p] = term[:, p * share : (p + 1) * share].astype(BF16)
+
+    send_all(fs_send, fs_all, fs_ss, fs_rs)
+    fs_all[me] = fs_send[me]
+    receive_all(fs_send, fs_all, fs_ss, fs_rs)
+    total = hid_s[me]
+    for s in range(count):
+        total = total + fs_all[s].astype(F32)
+    out_ref[...] = total.astype(BF16)
+
+    for d in range(1, groups):
+        exchange(d, q_send, q_all, q_ss, q_rs, True).wait_send()
+        exchange(d, log_send, log_all, log_ss, log_rs, True).wait_send()
+        exchange(d, part_send, part_all, part_ss, part_rs, True).wait_send()
+    sent_all(rs_send, rs_all, rs_ss, rs_rs)
+    sent_all(ag_send, ag_all, ag_ss, ag_rs)
+    sent_all(fs_send, fs_all, fs_ss, fs_rs)
+
+
+def per_device(*operands):
+    (hidden_in, queries_nope, queries_rope, cache, lengths, w_uk, w_uv, w_out, norm_gain,
+     w_gate, w_up, w_down) = operands
+    groups, tps = lax.axis_size("kvp"), lax.axis_size("tp")
+    count = groups * tps
+    batch, heads, head_dim = queries_nope.shape
+    latent, rope, ctx = w_uk.shape[2], queries_rope.shape[2], cache.shape[1]
+    width = hidden_in.shape[1]
+    share = width // count
+    ff = w_gate.shape[1]
+    rows = w_out.shape[0]
+    per_chunk = 1
+    while share * per_chunk % 128 and per_chunk < count:
+        per_chunk *= 2
+    chunk = share * per_chunk
+    held = (w_gate.size + w_up.size + max(rows, ff) * width + cache.size + w_uk.size + w_uv.size) * 2
+    fits = (
+        batch % 8 == 0
+        and heads % 8 == 0
+        and all(size % 128 == 0 for size in (head_dim, latent, ctx, chunk, ff))
+        and count % per_chunk == 0
+        and rows <= ff
+        and held < VMEM_BYTES - 8 * 2**20
+    )
+    if not fits:
+        return plain_device(*operands)
+    chunks = width // chunk
+    dma = pltpu.SemaphoreType.DMA
+    vmem = pl.BlockSpec(memory_space=pltpu.VMEM)
+    anywhere = pl.BlockSpec(memory_space=pl.ANY)
+    spread = pltpu.VMEM((count, batch, share), BF16)
+    scratch = [
+        pltpu.VMEM(cache.shape, BF16),
+        pltpu.VMEM(w_uk.shape, BF16),
+        pltpu.VMEM(w_uv.shape, BF16),
+        pltpu.VMEM((chunks, ff, chunk), BF16),
+        pltpu.VMEM(w_gate.shape, BF16),
+        pltpu.VMEM(w_up.shape, BF16),
+        pltpu.VMEM((batch, heads, head_dim), F32),
+        pltpu.VMEM((batch, heads, latent), F32),
+        pltpu.VMEM((batch, heads, latent + rope), BF16),
+        pltpu.VMEM((groups, batch, heads, latent + rope), BF16),
+        pltpu.VMEM((batch, groups * heads, ctx), F32),
+        pltpu.VMEM((groups, batch, heads, latent), BF16),
+        pltpu.VMEM((groups, batch, heads, latent), BF16),
+        pltpu.VMEM((groups, batch, heads, 128), F32),
+        pltpu.VMEM((groups, batch, heads, 128), F32),
+        pltpu.VMEM((batch, heads, latent), F32),
+        pltpu.VMEM((batch, heads * head_dim), BF16),
+        pltpu.VMEM((count, batch, share), F32),
+        spread,
+        spread,
+        pltpu.VMEM((batch, share), BF16),
+        spread,
+        pltpu.VMEM((batch, width), F32),
+        pltpu.VMEM((batch, width), BF16),
+        spread,
+        spread,
+        dma, dma, dma,
+        dma((chunks,)), dma((chunks,)), dma((chunks,)), dma((chunks,)),
+    ] + [dma((groups,))] * 6 + [dma((count,))] * 6
+    return pl.pallas_call(
+        functools.partial(layer_kernel, groups, tps, share, chunk, rows),
+        out_shape=jax.ShapeDtypeStruct((batch, share), BF16),
+        in_specs=[vmem, vmem, vmem, pl.BlockSpec(memory_space=pltpu.SMEM), vmem] + [anywhere] * 7,
+        out_specs=vmem,
+        scratch_shapes=scratch,
+        compiler_params=pltpu.CompilerParams(
+            collective_id=0, has_side_effects=True, vmem_limit_bytes=VMEM_BYTES
+        ),
+    )(
+        hidden_in, queries_nope, queries_rope, lengths, norm_gain.reshape(1, width),
+        cache, w_uk, w_uv, w_out, w_gate, w_up, w_down,
+    )
+
+
 def solution(mesh):
     placed = (
         P("grp", None),

time: 249 us -> 55.6 us (0.22)
  waiting for transfers between devices: 166 us -> 0 us
  Pallas kernels: 0 us -> 48.1 us
  matrix products: 40 us -> 0 us
  between operations: 13.5 us -> 0.01 us
  blocking collectives: 12.6 us -> 0 us
  starting transfers between devices: 6.74 us -> 0 us
  other arithmetic: 4.23 us -> 0 us
    psum x1 -> x0, waiting for transfers between devices: 89.8 us -> none  [per_device(): attn_whole = lax.psum(attention, ('kvp', 'tp'))]
    unnamed x3 -> x0, waiting for transfers between devices: 69.7 us -> none
    pallas_call x0 -> x1, Pallas kernels: none -> 48.1 us  [per_device(): pl.pallas_call(functools.partial(layer_kernel, groups, tps, share, chunk,...]
    dot_general x5 -> x0, matrix products: 21.4 us -> none  [the longest x1 8.58 us: per_device(): gate_proj = jnp.dot(normed, w_gate, preferred_element_type=jnp.float32)]
    unnamed x1 -> x0, matrix products: 18.6 us -> none
    all_gather x2 -> x0, blocking collectives: 12.6 us -> none  [the longest x1 6.3 us: per_device(): lax.all_gather(queries_rope, 'kvp', axis=1, tiled=True)]
    all_to_all x2 -> x0, starting transfers between devices: 6.65 us -> none  [the longest x1 3.4 us: per_device(): lax.all_to_all(blocks.astype(jnp.bfloat16), 'kvp', split_axis=1, concat_a...]
    all_to_all x2 -> x0, waiting for transfers between devices: 6.61 us -> none  [the longest x1 5.84 us: per_device(): lax.all_to_all(blocks.astype(jnp.bfloat16), 'kvp', split_axis=1, concat_a...]
  transfers between devices with their start and end apart: 4 -> 0, of which waited for: 4 -> 0; matrix products, arithmetic and copies ran while one was open for 1% -> 0% of each run, Pallas kernels for 0% -> 0%
where the time goes in v1:
time: 55.6 us; the launch traced here: 55.3 us
  Pallas kernels  48.1 us (87%)
  local copies, waits for them, and re-layouts  7.24 us (13%)
    pallas_call x1, Pallas kernels, per_device(): pl.pallas_call(functools.partial(layer_kernel, groups, tps, share, chunk,...  48.1 us
    unnamed x2, local copies, waits for them, and re-layouts  7.24 us

profile of v1, /device:TPU:0, one launch (start us, length us, event | category | flops | bytes accessed | tf_op | source)
XLA Modules:
  0.0 55.3 jit_solution(2922643923215803659)
XLA Ops:
  0.0 5.9 %copy.13.cache_hbm = bf16[8,384,576]{2,1,0:T(8,128)(2,1)} copy(bf16[8,384,576]{1,2,0:T(8,128)(2,1)} %param.15) | data formatting | bytes 7077888 | tf_op args[3]
  5.9 48.1 %shard_map.118 = bf16[8,448]{1,0:T(8,128)(2,1)} custom-call(bf16[8,7168]{1,0:T(8,128)(2,1)} %hidden_ref.1, bf16[8,8,128]{2,1,0:T(8,128)(2,1)} %nope_ref.1, bf16[8,8,64]{2,1,0:T(8,128)(2,1)} %rope_ref.1, s32[8]{0:T(128)} %len_ref.1, f32[1,7168]{1,0:T(1,128)} %bitcast.1, bf16[8,384,576]{2,1,0:T(8,128)(2,1)} %copy.13.cache_hbm, bf16[8,128,512]{2,1,0:T(8,128)(2,1)} %uk_hbm.1, ...), custom_call_target="tpu_custom_call" | custom-call | tf_op jit(solution)/shard_map/pallas_call | solution.py:410
  54.0 1.3 %copy.15 = bf16[8,448]{1,0:T(8,128)(2,1)} copy(bf16[8,448]{1,0:T(8,128)(2,1)} %shard_map.118) | data formatting | bytes 14336

commit v2 on v1

--- a/solution.py
+++ b/solution.py
@@ -115,13 +115,16 @@
     batch, heads, head_dim = nope_ref.shape
     latent = uk_v.shape[2]
     rope = rope_ref.shape[2]
-    ctx = cache_v.shape[1]
+    ctx = cache_v.shape[2]
     width = hidden_ref.shape[1]
     chunks = width // chunk
     per_chunk = chunk // share
 
     def peer(index):
         return {"kvp": index // tps, "tp": index % tps}
+
+    def turn(step):
+        return lax.rem(me // per_chunk + 1 + step, chunks)
 
     def load_uk():
         return pltpu.make_async_copy(uk_hbm, uk_v, uk_sem)
@@ -167,8 +170,8 @@
     load_uv().start()
 
     @pl.loop(0, chunks)
-    def _(j):
-        load_wo(j).start()
+    def _(step):
+        load_wo(turn(step)).start()
 
     for i in range(heads):
         qlat_s[:, i, :] = jnp.dot(
@@ -206,14 +209,13 @@
     rows = groups * heads
     for b in range(batch):
         q = q_all[:, b].astype(F32).reshape(rows, latent + rope)
-        contract = (((1,), (1,)), ((), ()))
         score_s[b] = (
-            lax.dot_general(
-                q[:, :latent].astype(BF16), cache_v[b, :, :latent], contract,
+            jnp.dot(
+                q[:, :latent].astype(BF16), cache_v[b, :latent],
                 preferred_element_type=F32,
             )
-            + lax.dot_general(
-                q[:, latent:].astype(BF16), cache_v[b, :, latent:], contract,
+            + jnp.dot(
+                q[:, latent:].astype(BF16), cache_v[b, latent:],
                 preferred_element_type=F32,
             )
         ) * scale
@@ -226,7 +228,9 @@
         guarded = jnp.maximum(jnp.sum(exps, axis=1, keepdims=True), 1.0)
         log_total = jnp.broadcast_to(top + jnp.log(guarded), (rows, 128))
         weights = (exps / guarded).astype(BF16)
-        part = jnp.dot(weights, cache_v[b, :, :latent], preferred_element_type=F32)
+        part = lax.dot_general(
+            weights, cache_v[b, :latent], (((1,), (1,)), ((), ())), preferred_element_type=F32
+        )
         for g in range(groups):
             part_send[g, b] = part[g * heads : (g + 1) * heads].astype(BF16)
             log_send[g, b] = log_total[g * heads : (g + 1) * heads]
@@ -265,6 +269,19 @@
             device_id_type=MESH,
         )
 
+    def send_chunk(j, term, source, target, ss, rs):
+        for p in range(per_chunk):
+            owner = j * per_chunk + p
+            source[owner] = term[:, p * share : (p + 1) * share].astype(BF16)
+        for p in range(per_chunk):
+            owner = j * per_chunk + p
+
+            @pl.when(owner != me)
+            def _():
+                scatter(
+                    lax.rem(owner - me + count, count), source, target, ss, rs, True
+                ).start()
+
     def send_all(source, target, ss, rs):
         @pl.loop(1, count)
         def _(d):
@@ -281,14 +298,13 @@
             scatter(d, source, target, ss, rs, True).wait_send()
 
     @pl.loop(0, chunks)
-    def _(j):
+    def _(step):
+        j = turn(step)
         load_wo(j).wait()
         term = jnp.dot(head_s[...], big_v[j, :out_rows], preferred_element_type=F32)
-        for p in range(per_chunk):
-            rs_send[j * per_chunk + p] = term[:, p * share : (p + 1) * share].astype(BF16)
         load_wd(j).start()
-
-    send_all(rs_send, rs_all, rs_ss, rs_rs)
+        send_chunk(j, term, rs_send, rs_all, rs_ss, rs_rs)
+
     rs_all[me] = rs_send[me]
     receive_all(rs_send, rs_all, rs_ss, rs_rs)
     residual = hid_s[me]
@@ -323,13 +339,12 @@
     act = (gate / (1.0 + jnp.exp(-gate)) * up).astype(BF16)
 
     @pl.loop(0, chunks)
-    def _(j):
+    def _(step):
+        j = turn(step)
         load_wd(j).wait()
         term = jnp.dot(act, big_v[j], preferred_element_type=F32)
-        for p in range(per_chunk):
-            fs_send[j * per_chunk + p] = term[:, p * share : (p + 1) * share].astype(BF16)
-
-    send_all(fs_send, fs_all, fs_ss, fs_rs)
+        send_chunk(j, term, fs_send, fs_all, fs_ss, fs_rs)
+
     fs_all[me] = fs_send[me]
     receive_all(fs_send, fs_all, fs_ss, fs_rs)
     total = hid_s[me]
@@ -378,7 +393,7 @@
     anywhere = pl.BlockSpec(memory_space=pl.ANY)
     spread = pltpu.VMEM((count, batch, share), BF16)
     scratch = [
-        pltpu.VMEM(cache.shape, BF16),
+        pltpu.VMEM((batch, latent + rope, ctx), BF16),
         pltpu.VMEM(w_uk.shape, BF16),
         pltpu.VMEM(w_uv.shape, BF16),
         pltpu.VMEM((chunks, ff, chunk), BF16),
@@ -418,7 +433,7 @@
         ),
     )(
         hidden_in, queries_nope, queries_rope, lengths, norm_gain.reshape(1, width),
-        cache, w_uk, w_uv, w_out, w_gate, w_up, w_down,
+        jnp.swapaxes(cache, 1, 2), w_uk, w_uv, w_out, w_gate, w_up, w_down,
     )
 
 

time: 55.6 us -> 46.3 us (0.83)
  local copies, waits for them, and re-layouts: 7.24 us -> 1.3 us
  Pallas kernels: 48.1 us -> 44.8 us
    unnamed x2 -> x1, local copies, waits for them, and re-layouts: 7.24 us -> 1.3 us
    pallas_call x1, Pallas kernels: 48.1 us -> 44.8 us  [per_device(): pl.pallas_call(functools.partial(layer_kernel, groups, tps, share, chunk,...]
where the time goes in v2:
time: 46.3 us; the launch traced here: 46.1 us
  Pallas kernels  44.8 us (97%)
  local copies, waits for them, and re-layouts  1.3 us (3%)
    pallas_call x1, Pallas kernels, per_device(): pl.pallas_call(functools.partial(layer_kernel, groups, tps, share, chunk,...  44.8 us
    unnamed x1, local copies, waits for them, and re-layouts  1.3 us

profile of v2, /device:TPU:0, one launch (start us, length us, event | category | flops | bytes accessed | tf_op | source)
XLA Modules:
  0.0 46.1 jit_solution(650407084910625536)
XLA Ops:
  0.0 44.8 %shard_map.118 = bf16[8,448]{1,0:T(8,128)(2,1)} custom-call(bf16[8,7168]{1,0:T(8,128)(2,1)} %hidden_ref.1, bf16[8,8,128]{2,1,0:T(8,128)(2,1)} %nope_ref.1, bf16[8,8,64]{2,1,0:T(8,128)(2,1)} %rope_ref.1, s32[8]{0:T(128)} %len_ref.1, f32[1,7168]{1,0:T(1,128)} %bitcast.3, bf16[8,576,384]{2,1,0:T(8,128)(2,1)} %bitcast.2, bf16[8,128,512]{2,1,0:T(8,128)(2,1)} %uk_hbm.1, ...), custom_call_target="tpu_custom_call" | custom-call | tf_op jit(solution)/shard_map/pallas_call | solution.py:425
  44.8 1.3 %copy.14 = bf16[8,448]{1,0:T(8,128)(2,1)} copy(bf16[8,448]{1,0:T(8,128)(2,1)} %shard_map.118) | data formatting | bytes 14336
